TPU v7x, 512 devices: a whole 4x8x8 slice. The times are simulated.
512 devices in a mesh: seq: 128 (over x, z, y_lo), head: 4 (over y_hi, core).
Axes of the slice: x: 4, y: 8 (y_hi: 2, y_lo: 4; y = y_hi * 4 + y_lo), z: 8, core: 2. Of those that a mesh axis runs over, the one named last changes fastest.
Arguments:
- features: bfloat16 [32768, 1024], P('seq', 'head'), may hold values from -6 to 6
- w_query: bfloat16 [1024, 512], P(None, 'head'), may hold values from -0.1875 to 0.1875
- w_key: bfloat16 [1024, 512], P(None, 'head'), may hold values from -0.1875 to 0.1875
- w_value: bfloat16 [1024, 1024], P(None, 'head'), may hold values from -0.1875 to 0.1875
- w_gate: bfloat16 [1024, 1024], P(None, 'head'), may hold values from -0.1875 to 0.1875
- w_out: bfloat16 [1024, 1024], replicated, may hold values from -0.1875 to 0.1875
- forget: bfloat16 [2, 32768, 512], P(None, 'seq', 'head'), may hold values from -2.5 to 0, as said below
Outputs:
- encoded: bfloat16 [32768, 1024], P('seq', 'head')
Inputs may be any that keep to these rules, and one draw needn't show every extreme that they name: `forget`: every entry is below zero.
All inputs are finite; a program needn't handle non-finite values.
Results may differ from a plain program's by a relative error of at most 0.013.
Values may be sent and summed in bfloat16 or wider, within the bound.
A program may use at most 64 MiB of HBM per device.

v0:
```python
import jax
import jax.numpy as jnp
from jax import lax
from jax.sharding import Mesh
from jax.sharding import PartitionSpec as P

HEAD_K = 64
HEAD_V = 128
GROUP = 64
SEQ = ("seq_0", "seq_1", "seq_2")


def from_everyone(shard, axis):
    copies = jnp.broadcast_to(shard, (lax.axis_size(axis), *shard.shape))
    return lax.all_to_all(copies, axis, split_axis=0, concat_axis=0, tiled=True)


def in_order(tiles, dim):
    dims = list(tiles.shape[1:])
    dims[dim] *= tiles.shape[0]
    return jnp.moveaxis(tiles, 0, dim).reshape(dims)


def collect(shard, axis, dim):
    tiles = from_everyone(shard, axis)
    return in_order(tiles, dim)


def nothing_yet(shard, identity):
    return jax.tree.map(
        lambda a, e: jnp.broadcast_to(jnp.asarray(e, a.dtype), a.shape), shard, identity
    )


def gathered_once(shard, axis):
    leaves = jax.tree.leaves(shard)
    order = sorted(range(len(leaves)), key=lambda k: -leaves[k].size)
    width = (1, *leaves[order[0]].shape)[-1]
    lines = [
        jnp.pad(leaves[k].reshape(-1), (0, -leaves[k].size % width)).reshape(-1, width)
        for k in order
    ]
    both, at, found = (lax.all_gather(jnp.concatenate(lines), axis), 0, {})
    for k, line in zip(order, lines):
        slab = both[:, at : at + len(line)].reshape(len(both), -1)
        found[k] = slab[:, : leaves[k].size].reshape(-1, *leaves[k].shape)
        at += len(line)
    numbers = iter(range(len(leaves)))
    return jax.tree.map(lambda _: found[next(numbers)], shard)


def prefix_by_axis(shard, axes, combine, identity):
    before = start = nothing_yet(shard, identity)
    so_far = shard
    for axis in reversed(axes):
        peers, place = (lax.axis_size(axis), lax.axis_index(axis))
        pieces = gathered_once(so_far, axis)
        inside, so_far = (start, start)
        for k in range(peers):
            passed = k < place
            so_far = combine(so_far, jax.tree.map(lambda part: part[k], pieces))
            inside = jax.tree.map(lambda new, old: jnp.where(passed, new, old), so_far, inside)
        before = combine(inside, before)
    return before


def carried_in(shard, axes, combine, identity):
    before = start = nothing_yet(shard, identity)
    so_far = shard
    for axis in reversed(axes):
        peers, place = (lax.axis_size(axis), lax.axis_index(axis))
        pieces = gathered_once(
            jax.tree.map(
                lambda part, kind: part.astype(kind), so_far, (jnp.bfloat16, jnp.bfloat16)
            ),
            axis,
        )
        inside, so_far = (start, start)
        for k in reversed(range(peers)):
            passed = k > place
            so_far = combine(
                so_far, jax.tree.map(lambda part, own: part[k].astype(own.dtype), pieces, shard)
            )
            inside = jax.tree.map(lambda new, old: jnp.where(passed, new, old), so_far, inside)
        before = combine(inside, before)
    return before


def to_blocks(tensor):
    block_count = tensor.shape[0] // GROUP
    return tensor.reshape((block_count, GROUP) + tensor.shape[1:])


def state_increment(memory, key_block, value_block, running):
    finale = running[-1]
    key_to_end = (key_block.astype(jnp.float32) * jnp.exp(finale[None] - running)).astype(
        jnp.bfloat16
    )
    added = jnp.einsum("shi,shj->hij", key_to_end, value_block, preferred_element_type=jnp.float32)
    return jnp.exp(finale)[:, :, None] * memory + added


def block_pass(query_matrix, key_rows, value_rows, decays, initial):
    triangle = jnp.tril(jnp.ones((GROUP, GROUP), jnp.float32))

    def block_advance(memory, blocks):
        query_block, key_block, value_block, decay_block = blocks
        running = jnp.cumsum(decay_block, axis=0)
        query_decayed = (query_block.astype(jnp.float32) * jnp.exp(running)).astype(jnp.bfloat16)
        key_grown = (key_block.astype(jnp.float32) * jnp.exp(-running)).astype(jnp.bfloat16)
        scores = (
            jnp.einsum("thi,shi->hts", query_decayed, key_grown, preferred_element_type=jnp.float32)
            * triangle
        )
        within = jnp.einsum(
            "hts,shj->thj",
            scores.astype(jnp.bfloat16),
            value_block,
            preferred_element_type=jnp.float32,
        )
        carried = jnp.einsum("thi,hij->thj", query_decayed.astype(jnp.float32), memory)
        memory = state_increment(memory, key_block, value_block, running)
        return (memory, within + carried)

    blocks = tuple((to_blocks(tensor) for tensor in (query_matrix, key_rows, value_rows, decays)))
    last_memory, outputs = lax.scan(block_advance, initial, blocks)
    return outputs.reshape((query_matrix.shape[0],) + outputs.shape[2:])


def device_summary(key_rows, value_rows, decays):
    heads_here = key_rows.shape[1]

    def device_advance(memory, blocks):
        key_block, value_block, decay_block = blocks
        running = jnp.cumsum(decay_block, axis=0)
        return (state_increment(memory, key_block, value_block, running), None)

    initial = jnp.zeros((heads_here, HEAD_K, HEAD_V), jnp.float32)
    memory, unused = lax.scan(
        device_advance,
        initial,
        tuple((to_blocks(tensor) for tensor in (key_rows, value_rows, decays))),
    )
    total = jnp.sum(decays, axis=0)
    return (total.reshape(-1), memory.reshape(-1, memory.shape[2]))


def combine_states(earlier, latter):
    return (earlier[0] + latter[0], jnp.exp(latter[0])[:, None] * earlier[1] + latter[1])


def local(features, w_query, w_key, w_value, w_gate, w_out, forget):
    row_count = features.shape[0]
    heads_here = w_query.shape[1] // HEAD_K
    columns = collect(features, "head", 1)
    query_sum, key_sum, value_sum, gating = tuple(
        (
            jnp.dot(columns, weight, preferred_element_type=jnp.float32)
            for weight in (w_query, w_key, w_value, w_gate)
        )
    )
    query_matrix = (query_sum * 0.125).astype(jnp.bfloat16).reshape(row_count, heads_here, HEAD_K)
    key_rows = key_sum.astype(jnp.bfloat16).reshape(row_count, heads_here, HEAD_K)
    value_rows = value_sum.astype(jnp.bfloat16).reshape(row_count, heads_here, HEAD_V)
    decays = forget.astype(jnp.float32).reshape(2, row_count, heads_here, HEAD_K)
    flipped_queries = jnp.flip(query_matrix, 0)
    flipped_keys = jnp.flip(key_rows, 0)
    flipped_values = jnp.flip(value_rows, 0)
    flipped_decays = jnp.flip(decays[1], 0)
    ahead_total, ahead_memory = device_summary(key_rows, value_rows, decays[0])
    behind_total, behind_memory = device_summary(flipped_keys, flipped_values, flipped_decays)
    identity = (jnp.zeros_like(ahead_total), jnp.zeros_like(ahead_memory))
    ahead_inflow = prefix_by_axis((ahead_total, ahead_memory), SEQ, combine_states, identity)[1]
    behind_inflow = carried_in((behind_total, behind_memory), SEQ, combine_states, identity)[1]
    ahead_out = block_pass(
        query_matrix,
        key_rows,
        value_rows,
        decays[0],
        ahead_inflow.reshape(heads_here, HEAD_K, HEAD_V),
    )
    behind_flipped = block_pass(
        flipped_queries,
        flipped_keys,
        flipped_values,
        flipped_decays,
        behind_inflow.reshape(heads_here, HEAD_K, HEAD_V),
    )
    mixture = ahead_out + jnp.flip(behind_flipped, 0)
    scaled = mixture * lax.rsqrt(jnp.mean(mixture * mixture, axis=-1, keepdims=True) + 1e-06)
    normed = (scaled.reshape(row_count, heads_here * HEAD_V) * jax.nn.silu(gating)).astype(
        jnp.bfloat16
    )
    out_width = w_out.shape[1] // lax.axis_size("head")
    own_columns = lax.dynamic_slice_in_dim(w_out, lax.axis_index("head") * out_width, out_width, 1)
    encoded = jnp.dot(
        lax.all_gather(normed, "head", axis=1, tiled=True),
        own_columns,
        preferred_element_type=jnp.float32,
    )
    return encoded.astype(jnp.bfloat16)


def solution(mesh):
    torus = Mesh(
        mesh.devices.reshape(4, 8, 4, mesh.shape["head"]), ("seq_0", "seq_1", "seq_2", "head")
    )
    placed = (
        P(SEQ, "head"),
        P(None, "head"),
        P(None, "head"),
        P(None, "head"),
        P(None, "head"),
        P(),
        P(None, SEQ, "head"),
    )
    return jax.shard_map(
        local, mesh=torus, in_specs=placed, out_specs=P(SEQ, "head"), check_vma=False
    )
```

profile of v0, /device:TPU:1, one launch (start us, length us, event | category | flops | bytes accessed | tf_op | source)
XLA Modules:
  0.0 234.6 jit_solution(15789298678491646530)
XLA Ops:
  0.0 1.2 copy.58
  1.2 0.8 broadcast_in_dim.16
  2.0 10.3 %all-to-all-start = ((bf16[4,256,256]{1,2,0:T(8,128)(2,1)}), bf16[4,256,256]{1,2,0:T(8,128)(2,1)S(1)}, u32[]{:S(2)}, u32[]{:S(2)}) async-start(bf16[4,256,256]{1,2,0:T(8,128)(2,1)} %broadcast_in_dim.16), calls=%async_computation | async-start | bytes 1048576 | tf_op jit(solution)/shard_map/all_to_all | solution.py:15
  14.0 1.0 slice_reduce_fusion
  15.0 11.3 %all-to-all-done = bf16[4,256,256]{1,2,0:T(8,128)(2,1)S(1)} async-done(((bf16[4,256,256]{1,2,0:T(8,128)(2,1)}), bf16[4,256,256]{1,2,0:T(8,128)(2,1)S(1)}, u32[]{:S(2)}, u32[]{:S(2)}) %all-to-all-start) | async-done | bytes 524320 | tf_op jit(solution)/shard_map/all_to_all | solution.py:15
  26.3 1.4 convolution_convert_fusion.1
  27.7 0.9 reshape.1405
  28.6 1.2 convolution_convert_fusion.2
  31.3 2.8 %rev.21 = bf16[256,2,128]{2,0,1:T(8,128)(2,1)} reverse(bf16[256,2,128]{2,0,1:T(8,128)(2,1)} %copy.69), dimensions={0} | reverse | bytes 262144 | tf_op jit(solution)/shard_map/jit(_flip)/rev | solution.py:168
  34.1 0.9 copy.71
  36.0 4.5 %while.51 = (s32[]{:T(128)}, f32[2,64,128]{2,1,0:T(8,128)S(1)}, f32[4,64,2,64]{3,2,1,0:T(2,128)S(1)}, bf16[4,64,2,64]{3,2,1,0:T(2,128)(2,1)}, bf16[4,64,2,128]{3,1,2,0:T(8,128)(2,1)S(1)}, /*index=5*/s32[]{:T(128)}, s32[]{:T(128)}) while((s32[]{:T(128)}, f32[2,64,128]{2,1,0:T(8,128)S(1)}, f32[4,64,2,64]{3,2,1,0:T(2,128)S(1)}, ...), condition=%wide.region_9.10_spmd.clone, body=%wide.region_7.9_spmd.clone.sunk | while | flops 2695171 | bytes 364131 | solution.py:139
  37.2 0.8 fusion.286
  40.6 11.2 %all-gather.9 = bf16[4,129,128]{2,1,0:T(8,128)(2,1)S(1)} all-gather(bf16[1,129,128]{2,1,0:T(8,128)(2,1)S(1)} %maximum_bitcast_fusion.3), channel_id=5, replica_groups=mesh['seq_0'=4,'seq_1'=8,'seq_2'=4,'head'=4] {'seq_2'}, dimensions={0}, use_global_device_ids=true | all-gather | bytes 165120 | tf_op jit(solution)/shard_map/all_gather | solution.py:43
  51.8 1.2 fusion.185
  53.1 25.6 %all-gather.10 = bf16[8,129,128]{2,1,0:T(8,128)(2,1)S(1)} all-gather(bf16[1,129,128]{2,1,0:T(8,128)(2,1)S(1)} %maximum_bitcast_fusion.4), channel_id=6, replica_groups=mesh['seq_0'=4,'seq_1'=8,'seq_2'=4,'head'=4] {'seq_1'}, dimensions={0}, use_global_device_ids=true | all-gather | bytes 297216 | tf_op jit(solution)/shard_map/all_gather | solution.py:43
  80.0 1.7 copy.62
  81.8 1.7 copy.61
  83.5 7.6 %while.50 = (s32[]{:T(128)}, f32[2,64,128]{2,1,0:T(8,128)S(1)}, f32[4,64,2,64]{3,2,1,0:T(2,128)S(1)}, bf16[4,64,2,64]{3,2,1,0:T(2,128)(2,1)}, bf16[4,64,2,128]{3,1,2,0:T(8,128)(2,1)}, /*index=5*/s32[]{:T(128)}, s32[]{:T(128)}) while((s32[]{:T(128)}, f32[2,64,128]{2,1,0:T(8,128)S(1)}, f32[4,64,2,64]{3,2,1,0:T(2,128)S(1)}, ...), condition=%wide.region_2.3_spmd.clone, body=%wide.region_0.2_spmd.clone.sunk | while | flops 2695171 | bytes 347743 | solution.py:139
  83.6 0.8 fusion.280
  84.4 1.0 convolution_add_fusion.10
  85.5 0.8 fusion.280
  86.3 1.0 convolution_add_fusion.10
  87.4 0.8 fusion.280
  88.2 1.0 convolution_add_fusion.10
  89.3 0.8 fusion.280
  90.2 1.0 convolution_add_fusion.10
  91.1 11.0 %all-gather.6 = f32[4,129,128]{2,1,0:T(8,128)S(1)} all-gather(f32[1,129,128]{2,1,0:T(8,128)S(1)} %maximum_bitcast_fusion), channel_id=2, replica_groups=mesh['seq_0'=4,'seq_1'=8,'seq_2'=4,'head'=4] {'seq_2'}, dimensions={0}, use_global_device_ids=true | all-gather | bytes 330240 | tf_op jit(solution)/shard_map/all_gather | solution.py:43
  102.8 1.7 slice_convert_fusion.7
  104.7 19.2 %all-gather.7 = f32[8,129,128]{2,1,0:T(8,128)S(1)} all-gather(f32[1,129,128]{2,1,0:T(8,128)S(1)} %maximum_bitcast_fusion.1), channel_id=3, replica_groups=mesh['seq_0'=4,'seq_1'=8,'seq_2'=4,'head'=4] {'seq_1'}, dimensions={0}, use_global_device_ids=true | all-gather | bytes 594432 | tf_op jit(solution)/shard_map/all_gather | solution.py:43
  125.0 10.0 %all-gather.8 = f32[4,129,128]{2,1,0:T(8,128)S(1)} all-gather(f32[1,129,128]{2,1,0:T(8,128)S(1)} %maximum_bitcast_fusion.2), channel_id=4, replica_groups=mesh['seq_0'=4,'seq_1'=8,'seq_2'=4,'head'=4] {'seq_0'}, dimensions={0}, use_global_device_ids=true | all-gather | bytes 330240 | tf_op jit(solution)/shard_map/all_gather | solution.py:43
  135.9 9.3 %all-gather.11 = bf16[4,129,128]{2,1,0:T(8,128)(2,1)S(1)} all-gather(bf16[1,129,128]{2,1,0:T(8,128)(2,1)S(1)} %maximum_bitcast_fusion.5), channel_id=7, replica_groups=mesh['seq_0'=4,'seq_1'=8,'seq_2'=4,'head'=4] {'seq_0'}, dimensions={0}, use_global_device_ids=true | all-gather | bytes 165120 | tf_op jit(solution)/shard_map/all_gather | solution.py:43
  148.7 1.2 fusion.76
  150.9 1.6 add_add_fusion
  153.2 15.1 %while.48 = (s32[]{:T(128)}, f32[2,64,128]{2,1,0:T(8,128)S(1)}, f32[4,64,2,128]{3,1,0,2:T(8,128)}, f32[4,64,2,64]{3,2,1,0:T(2,128)S(1)}, bf16[4,64,2,64]{3,2,1,0...) while((s32[]{:T(128)}, f32[2,64,128]{2,1,0:T(8,128)S(1)}, ...), condition=%wide.region_6.7_spmd.clone, body=%wide.region_4.6_spmd.clone.sunk | while | flops 8011778 | bytes 774749 | solution.py:126
  153.3 0.9 fusion.259
  154.4 1.6 fusion.262
  156.0 1.0 convolution_add_fusion.8
  157.1 0.9 fusion.259
  158.2 1.6 fusion.262
  159.8 1.0 convolution_add_fusion.8
  160.9 0.9 fusion.259
  161.9 1.6 fusion.262
  163.6 1.0 convolution_add_fusion.8
  164.7 0.9 fusion.259
  165.7 1.6 fusion.262
  167.4 1.0 convolution_add_fusion.8
  179.2 1.6 fusion.81
  181.4 15.1 %while.49 = (s32[]{:T(128)}, f32[2,64,128]{2,1,0:T(8,128)S(1)}, f32[4,64,2,128]{3,1,0,2:T(8,128)}, f32[4,64,2,64]{3,2,1,0:T(2,128)S(1)}, bf16[4,64,2,64]{3,2,1,0...) while((s32[]{:T(128)}, f32[2,64,128]{2,1,0:T(8,128)S(1)}, ...), condition=%wide.region_13.14_spmd.clone, body=%wide.region_11.13_spmd.clone.sunk | while | flops 8011778 | bytes 774749 | solution.py:126
  181.5 0.9 fusion.272
  182.6 1.6 fusion.275
  184.2 1.0 convolution_add_fusion.9
  185.3 0.9 fusion.272
  186.3 1.6 fusion.275
  188.0 1.0 convolution_add_fusion.9
  189.1 0.9 fusion.272
  190.1 1.6 fusion.275
  191.8 1.0 convolution_add_fusion.9
  192.8 0.9 fusion.272
  193.9 1.6 fusion.275
  195.5 1.0 convolution_add_fusion.9
  196.5 1.7 rev.23
  198.6 1.4 fusion.78
  200.0 33.7 %all_gather.51 = bf16[256,1024]{1,0:T(8,128)(2,1)S(1)} all-gather(bf16[256,256]{1,0:T(8,128)(2,1)S(1)} %fusion.78), channel_id=1, replica_groups=mesh['seq_0'=4,'seq_1'=8,'seq_2'=4,'head'=4] {'head'}, dimensions={1}, use_global_device_ids=true | all-gather | bytes 655360 | tf_op jit(solution)/shard_map/all_gather | solution.py:197
  233.7 1.0 convolution_convert_fusion
  (178 shorter events, 31.2 us)
Async XLA Ops:
  0.0 233.7 %copy-start = (bf16[1024,1024]{1,0:T(8,128)(2,1)S(1)}, bf16[1024,1024]{1,0:T(8,128)(2,1)}, u32[]{:S(2)}) copy-start(bf16[1024,1024]{1,0:T(8,128)(2,1)} %param.20) | copy-start | bytes 6291460
  0.0 12.3 %copy-start.5 = (bf16[2,256,128]{2,1,0:T(8,128)(2,1)S(1)}, bf16[2,256,128]{2,1,0:T(8,128)(2,1)}, u32[]{:S(2)}) copy-start(bf16[2,256,128]{2,1,0:T(8,128)(2,1)} %param.21) | copy-start | bytes 393220
  2.0 24.3 %all-to-all-start = ((bf16[4,256,256]{1,2,0:T(8,128)(2,1)}), bf16[4,256,256]{1,2,0:T(8,128)(2,1)S(1)}, u32[]{:S(2)}, u32[]{:S(2)}) async-start(bf16[4,256,256]{1,2,0:T(8,128)(2,1)} %broadcast_in_dim.16), calls=%async_computation | async-start | bytes 1048576 | tf_op jit(solution)/shard_map/all_to_all | solution.py:15
  40.6 50.6 %copy-start.1 = (bf16[4,64,2,128]{3,1,2,0:T(8,128)(2,1)}, bf16[4,64,2,128]{3,1,2,0:T(8,128)(2,1)S(1)}, u32[]{:S(2)}) copy-start(bf16[4,64,2,128]{3,1,2,0:T(8,128)(2,1)S(1)} %get-tuple-element.688) | copy-start | bytes 393220
  78.7 0.7 copy-start.2
  104.5 31.2 %copy-start.3 = (bf16[8,129,128]{2,1,0:T(8,128)(2,1)S(1)}, bf16[8,129,128]{2,1,0:T(8,128)(2,1)}, u32[]{:S(2)}) copy-start(bf16[8,129,128]{2,1,0:T(8,128)(2,1)} %copy-done.2) | copy-start | bytes 792580
  104.5 31.4 %copy-start.6 = (bf16[1,128]{1,0:T(2,128)(2,1)S(1)}, bf16[1,128]{1,0:T(2,128)(2,1)}, u32[]{:S(2)}) copy-start(bf16[1,128]{1,0:T(2,128)(2,1)} %convert_bitcast_fusion) | copy-start | bytes 772
  153.2 18.0 %copy-start.7 = (f32[1,1,128]{2,1,0:T(1,128)S(1)}, f32[1,1,128]{2,1,0:T(1,128)}, u32[]{:S(2)}) copy-start(f32[1,1,128]{2,1,0:T(1,128)} %get-tuple-element.415) | copy-start | bytes 1540
  153.2 24.7 %copy-start.10 = (f32[128]{0:T(128)S(1)}, f32[128]{0:T(128)}, u32[]{:S(2)}) copy-start(f32[128]{0:T(128)} %get-tuple-element.307) | copy-start | bytes 1540
  153.2 24.8 %copy-start.9 = (f32[128]{0:T(128)S(1)}, f32[128]{0:T(128)}, u32[]{:S(2)}) copy-start(f32[128]{0:T(128)} %get-tuple-element.308) | copy-start | bytes 1540
  153.2 24.8 %copy-start.8 = (f32[128]{0:T(128)S(1)}, f32[128]{0:T(128)}, u32[]{:S(2)}) copy-start(f32[128]{0:T(128)} %get-tuple-element.306) | copy-start | bytes 1540
  181.4 16.8 %copy-start.4 = (f32[4,64,2,128]{3,1,0,2:T(8,128)S(1)}, f32[4,64,2,128]{3,1,0,2:T(8,128)}, u32[]{:S(2)}) copy-start(f32[4,64,2,128]{3,1,0,2:T(8,128)} %get-tuple-element.144) | copy-start | bytes 786436
where the time goes:
time: 238 us; the launch traced here: 235 us
  blocking collectives  120 us (50%)
  matrix products  32.7 us (14%)
  local copies, waits for them, and re-layouts  32.1 us (13%)
  other arithmetic  27.5 us (12%)
  waiting for transfers between devices  11.3 us (5%)
  starting transfers between devices  10.3 us (4%)
    all_gather x6, blocking collectives, gathered_once(): both, at, found = (lax.all_gather(jnp.concatenate(lines), axis), 0, {})  86.3 us
    all_gather x1, blocking collectives, local(): lax.all_gather(normed, 'head', axis=1, tiled=True)  33.7 us
    dot_general x8, matrix products, block_advance(): jnp.einsum('hts,shj->thj', scores.astype(jnp.bfloat16), value_block, pref...  13.2 us
    dot_general x16, matrix products, state_increment(): jnp.einsum('shi,shj->hij', key_to_end, value_block, preferred_element_typ...  12.3 us
    all_to_all x1, waiting for transfers between devices, from_everyone(): return lax.all_to_all(copies, axis, split_axis=0, concat_axis=0, tiled=True)  11.3 us
    all_to_all x1, starting transfers between devices, from_everyone(): return lax.all_to_all(copies, axis, split_axis=0, concat_axis=0, tiled=True)  10.3 us
    exp x31, local copies, waits for them, and re-layouts, combine_states(): jnp.exp(latter[0])[:, None] * earlier[1] + latter[1]  9.35 us
    convert_element_type x8, other arithmetic, block_advance(): (key_block.astype(jnp.float32) * jnp.exp(-running)).astype(jnp.bfloat16)  7.31 us
  transfers between devices with their start and end apart: 1, of which 1 were waited for; matrix products, arithmetic and copies ran while one was open for 1% of the time, Pallas kernels for 0%

commit v1 on v0

--- a/solution.py
+++ b/solution.py
@@ -194,7 +194,9 @@
     out_width = w_out.shape[1] // lax.axis_size("head")
     own_columns = lax.dynamic_slice_in_dim(w_out, lax.axis_index("head") * out_width, out_width, 1)
     encoded = jnp.dot(
-        lax.all_gather(normed, "head", axis=1, tiled=True),
+        jnp.concatenate(
+            lax.all_to_all(jnp.stack([normed] * lax.axis_size("head")), "head", 0, 0), axis=1
+        ),
         own_columns,
         preferred_element_type=jnp.float32,
     )

time: 238 us -> 248 us (1.042)
  the two profiles are of different devices: /device:TPU:1 before, /device:TPU:8 now
where the time goes in v1:
time: 248 us; the launch traced here: 244 us
  blocking collectives  107 us (43%)
  waiting for transfers between devices  33.9 us (14%)
  local copies, waits for them, and re-layouts  32.8 us (13%)
  matrix products  32.7 us (13%)
  other arithmetic  27.3 us (11%)
  starting transfers between devices  9.66 us (4%)
    all_gather x6, blocking collectives, gathered_once(): both, at, found = (lax.all_gather(jnp.concatenate(lines), axis), 0, {})  107 us
    all_to_all x1, waiting for transfers between devices, local(): lax.all_to_all(jnp.stack([normed] * lax.axis_size('head')), 'head', 0, 0)  18.3 us
    all_to_all x1, waiting for transfers between devices, from_everyone(): return lax.all_to_all(copies, axis, split_axis=0, concat_axis=0, tiled=True)  15.6 us
    dot_general x8, matrix products, block_advance(): jnp.einsum('hts,shj->thj', scores.astype(jnp.bfloat16), value_block, pref...  13.2 us
    dot_general x16, matrix products, state_increment(): jnp.einsum('shi,shj->hij', key_to_end, value_block, preferred_element_typ...  12.3 us
    exp x31, local copies, waits for them, and re-layouts, combine_states(): jnp.exp(latter[0])[:, None] * earlier[1] + latter[1]  9.23 us
    convert_element_type x8, other arithmetic, block_advance(): (key_block.astype(jnp.float32) * jnp.exp(-running)).astype(jnp.bfloat16)  7.31 us
    unnamed x30, local copies, waits for them, and re-layouts  6.88 us
  transfers between devices with their start and end apart: 2, of which 2 were waited for; matrix products, arithmetic and copies ran while one was open for 1% of the time, Pallas kernels for 0%

profile of v1, /device:TPU:8, one launch (start us, length us, event | category | flops | bytes accessed | tf_op | source)
XLA Modules:
  0.0 244.3 jit_solution(8620672456260527433)
XLA Ops:
  0.0 1.2 copy.59
  1.2 0.8 broadcast_in_dim.16
  2.0 6.2 %all-to-all-start = ((bf16[4,256,256]{1,2,0:T(8,128)(2,1)}), bf16[4,256,256]{1,2,0:T(8,128)(2,1)S(1)}, u32[]{:S(2)}, u32[]{:S(2)}) async-start(bf16[4,256,256]{1,2,0:T(8,128)(2,1)} %broadcast_in_dim.16), calls=%async_computation | async-start | bytes 1048576 | tf_op jit(solution)/shard_map/all_to_all | solution.py:15
  9.9 1.0 slice_reduce_fusion
  10.9 15.6 %all-to-all-done = bf16[4,256,256]{1,2,0:T(8,128)(2,1)S(1)} async-done(((bf16[4,256,256]{1,2,0:T(8,128)(2,1)}), bf16[4,256,256]{1,2,0:T(8,128)(2,1)S(1)}, u32[]{:S(2)}, u32[]{:S(2)}) %all-to-all-start) | async-done | bytes 524320 | tf_op jit(solution)/shard_map/all_to_all | solution.py:15
  26.5 1.4 convolution_convert_fusion.1
  27.9 0.9 reshape.1415
  28.8 1.2 convolution_convert_fusion.2
  31.6 2.8 %rev.21 = bf16[256,2,128]{2,0,1:T(8,128)(2,1)} reverse(bf16[256,2,128]{2,0,1:T(8,128)(2,1)} %copy.70), dimensions={0} | reverse | bytes 262144 | tf_op jit(solution)/shard_map/jit(_flip)/rev | solution.py:168
  34.3 0.9 copy.72
  36.2 4.5 %while.51 = (s32[]{:T(128)}, f32[2,64,128]{2,1,0:T(8,128)S(1)}, f32[4,64,2,64]{3,2,1,0:T(2,128)S(1)}, bf16[4,64,2,64]{3,2,1,0:T(2,128)(2,1)}, bf16[4,64,2,128]{3,1,2,0:T(8,128)(2,1)S(1)}, /*index=5*/s32[]{:T(128)}, s32[]{:T(128)}) while((s32[]{:T(128)}, f32[2,64,128]{2,1,0:T(8,128)S(1)}, f32[4,64,2,64]{3,2,1,0:T(2,128)S(1)}, ...), condition=%wide.region_9.10_spmd.clone, body=%wide.region_7.9_spmd.clone.sunk | while | flops 2695171 | bytes 364131 | solution.py:139
  40.8 11.9 %all-gather.9 = bf16[4,129,128]{2,1,0:T(8,128)(2,1)S(1)} all-gather(bf16[1,129,128]{2,1,0:T(8,128)(2,1)S(1)} %maximum_bitcast_fusion.3), channel_id=5, replica_groups=mesh['seq_0'=4,'seq_1'=8,'seq_2'=4,'head'=4] {'seq_2'}, dimensions={0}, use_global_device_ids=true | all-gather | bytes 165120 | tf_op jit(solution)/shard_map/all_gather | solution.py:43
  52.7 1.2 fusion.185
  54.1 31.2 %all-gather.10 = bf16[8,129,128]{2,1,0:T(8,128)(2,1)S(1)} all-gather(bf16[1,129,128]{2,1,0:T(8,128)(2,1)S(1)} %maximum_bitcast_fusion.4), channel_id=6, replica_groups=mesh['seq_0'=4,'seq_1'=8,'seq_2'=4,'head'=4] {'seq_1'}, dimensions={0}, use_global_device_ids=true | all-gather | bytes 297216 | tf_op jit(solution)/shard_map/all_gather | solution.py:43
  86.5 1.7 copy.63
  88.3 1.7 copy.62
  90.0 7.6 %while.50 = (s32[]{:T(128)}, f32[2,64,128]{2,1,0:T(8,128)S(1)}, f32[4,64,2,64]{3,2,1,0:T(2,128)S(1)}, bf16[4,64,2,64]{3,2,1,0:T(2,128)(2,1)}, bf16[4,64,2,128]{3,1,2,0:T(8,128)(2,1)}, /*index=5*/s32[]{:T(128)}, s32[]{:T(128)}) while((s32[]{:T(128)}, f32[2,64,128]{2,1,0:T(8,128)S(1)}, f32[4,64,2,64]{3,2,1,0:T(2,128)S(1)}, ...), condition=%wide.region_2.3_spmd.clone, body=%wide.region_0.2_spmd.clone.sunk | while | flops 2695171 | bytes 347743 | solution.py:139
  90.9 1.0 convolution_add_fusion.10
  92.0 0.8 fusion.280
  92.8 1.0 convolution_add_fusion.10
  93.9 0.8 fusion.280
  94.7 1.0 convolution_add_fusion.10
  95.8 0.8 fusion.280
  96.6 1.0 convolution_add_fusion.10
  97.6 13.9 %all-gather.6 = f32[4,129,128]{2,1,0:T(8,128)S(1)} all-gather(f32[1,129,128]{2,1,0:T(8,128)S(1)} %maximum_bitcast_fusion), channel_id=2, replica_groups=mesh['seq_0'=4,'seq_1'=8,'seq_2'=4,'head'=4] {'seq_2'}, dimensions={0}, use_global_device_ids=true | all-gather | bytes 330240 | tf_op jit(solution)/shard_map/all_gather | solution.py:43
  112.2 1.7 slice_convert_fusion.7
  114.1 25.3 %all-gather.7 = f32[8,129,128]{2,1,0:T(8,128)S(1)} all-gather(f32[1,129,128]{2,1,0:T(8,128)S(1)} %maximum_bitcast_fusion.1), channel_id=3, replica_groups=mesh['seq_0'=4,'seq_1'=8,'seq_2'=4,'head'=4] {'seq_1'}, dimensions={0}, use_global_device_ids=true | all-gather | bytes 594432 | tf_op jit(solution)/shard_map/all_gather | solution.py:43
  140.5 12.6 %all-gather.8 = f32[4,129,128]{2,1,0:T(8,128)S(1)} all-gather(f32[1,129,128]{2,1,0:T(8,128)S(1)} %maximum_bitcast_fusion.2), channel_id=4, replica_groups=mesh['seq_0'=4,'seq_1'=8,'seq_2'=4,'head'=4] {'seq_0'}, dimensions={0}, use_global_device_ids=true | all-gather | bytes 330240 | tf_op jit(solution)/shard_map/all_gather | solution.py:43
  154.0 12.0 %all-gather.11 = bf16[4,129,128]{2,1,0:T(8,128)(2,1)S(1)} all-gather(bf16[1,129,128]{2,1,0:T(8,128)(2,1)S(1)} %maximum_bitcast_fusion.5), channel_id=7, replica_groups=mesh['seq_0'=4,'seq_1'=8,'seq_2'=4,'head'=4] {'seq_0'}, dimensions={0}, use_global_device_ids=true | all-gather | bytes 165120 | tf_op jit(solution)/shard_map/all_gather | solution.py:43
  169.5 1.2 fusion.76
  171.6 1.6 add_add_fusion
  174.0 15.1 %while.48 = (s32[]{:T(128)}, f32[2,64,128]{2,1,0:T(8,128)S(1)}, f32[4,64,2,128]{3,1,0,2:T(8,128)}, f32[4,64,2,64]{3,2,1,0:T(2,128)S(1)}, bf16[4,64,2,64]{3,2,1,0...) while((s32[]{:T(128)}, f32[2,64,128]{2,1,0:T(8,128)S(1)}, ...), condition=%wide.region_6.7_spmd.clone, body=%wide.region_4.6_spmd.clone.sunk | while | flops 8011778 | bytes 774749 | solution.py:126
  174.1 0.9 fusion.259
  175.1 1.6 fusion.262
  176.8 1.0 convolution_add_fusion.8
  177.8 0.9 fusion.259
  178.9 1.6 fusion.262
  180.6 1.0 convolution_add_fusion.8
  181.6 0.9 fusion.259
  182.7 1.6 fusion.262
  184.3 1.0 convolution_add_fusion.8
  185.4 0.9 fusion.259
  186.5 1.6 fusion.262
  188.1 1.0 convolution_add_fusion.8
  199.7 1.6 fusion.81
  202.0 15.1 %while.49 = (s32[]{:T(128)}, f32[2,64,128]{2,1,0:T(8,128)S(1)}, f32[4,64,2,128]{3,1,0,2:T(8,128)}, f32[4,64,2,64]{3,2,1,0:T(2,128)S(1)}, bf16[4,64,2,64]{3,2,1,0...) while((s32[]{:T(128)}, f32[2,64,128]{2,1,0:T(8,128)S(1)}, ...), condition=%wide.region_13.14_spmd.clone, body=%wide.region_11.13_spmd.clone.sunk | while | flops 8011778 | bytes 774749 | solution.py:126
  202.1 0.9 fusion.272
  203.1 1.6 fusion.275
  204.8 1.0 convolution_add_fusion.9
  205.8 0.9 fusion.272
  206.9 1.6 fusion.275
  208.5 1.0 convolution_add_fusion.9
  209.6 0.9 fusion.272
  210.7 1.6 fusion.275
  212.3 1.0 convolution_add_fusion.9
  213.4 0.9 fusion.272
  214.4 1.6 fusion.275
  216.1 1.0 convolution_add_fusion.9
  217.1 1.7 rev.23
  219.1 1.4 fusion.78
  220.6 0.8 stack.2
  221.5 3.5 %all-to-all-start.1 = ((bf16[4,256,256]{1,2,0:T(8,128)(2,1)}), bf16[4,256,256]{1,2,0:T(8,128)(2,1)S(1)}, u32[]{:S(2)}, u32[]{:S(2)}) async-start(bf16[4,256,256]{1,2,0:T(8,128)(2,1)} %stack.2), calls=%async_computation.1 | async-start | bytes 1048576 | tf_op jit(solution)/shard_map/all_to_all | solution.py:198
  224.9 18.3 %all-to-all-done.1 = bf16[4,256,256]{1,2,0:T(8,128)(2,1)S(1)} async-done(((bf16[4,256,256]{1,2,0:T(8,128)(2,1)}), bf16[4,256,256]{1,2,0:T(8,128)(2,1)S(1)}, u32[]{:S(2)}, u32[]{:S(2)}) %all-to-all-start.1) | async-done | bytes 524320 | tf_op jit(solution)/shard_map/all_to_all | solution.py:198
  243.2 1.0 convolution_convert_fusion
  (181 shorter events, 32.6 us)
Async XLA Ops:
  0.0 243.2 %copy-start = (bf16[1024,1024]{1,0:T(8,128)(2,1)S(1)}, bf16[1024,1024]{1,0:T(8,128)(2,1)}, u32[]{:S(2)}) copy-start(bf16[1024,1024]{1,0:T(8,128)(2,1)} %param.20) | copy-start | bytes 6291460
  0.0 8.2 %copy-start.5 = (bf16[2,256,128]{2,1,0:T(8,128)(2,1)S(1)}, bf16[2,256,128]{2,1,0:T(8,128)(2,1)}, u32[]{:S(2)}) copy-start(bf16[2,256,128]{2,1,0:T(8,128)(2,1)} %param.21) | copy-start | bytes 393220
  2.0 24.5 %all-to-all-start = ((bf16[4,256,256]{1,2,0:T(8,128)(2,1)}), bf16[4,256,256]{1,2,0:T(8,128)(2,1)S(1)}, u32[]{:S(2)}, u32[]{:S(2)}) async-start(bf16[4,256,256]{1,2,0:T(8,128)(2,1)} %broadcast_in_dim.16), calls=%async_computation | async-start | bytes 1048576 | tf_op jit(solution)/shard_map/all_to_all | solution.py:15
  40.8 56.8 %copy-start.1 = (bf16[4,64,2,128]{3,1,2,0:T(8,128)(2,1)}, bf16[4,64,2,128]{3,1,2,0:T(8,128)(2,1)S(1)}, u32[]{:S(2)}) copy-start(bf16[4,64,2,128]{3,1,2,0:T(8,128)(2,1)S(1)} %get-tuple-element.688) | copy-start | bytes 393220
  85.3 0.7 copy-start.2
  113.9 39.9 %copy-start.3 = (bf16[8,129,128]{2,1,0:T(8,128)(2,1)S(1)}, bf16[8,129,128]{2,1,0:T(8,128)(2,1)}, u32[]{:S(2)}) copy-start(bf16[8,129,128]{2,1,0:T(8,128)(2,1)} %copy-done.2) | copy-start | bytes 792580
  113.9 40.1 %copy-start.6 = (bf16[1,128]{1,0:T(2,128)(2,1)S(1)}, bf16[1,128]{1,0:T(2,128)(2,1)}, u32[]{:S(2)}) copy-start(bf16[1,128]{1,0:T(2,128)(2,1)} %convert_bitcast_fusion) | copy-start | bytes 772
  174.0 17.9 %copy-start.7 = (f32[1,1,128]{2,1,0:T(1,128)S(1)}, f32[1,1,128]{2,1,0:T(1,128)}, u32[]{:S(2)}) copy-start(f32[1,1,128]{2,1,0:T(1,128)} %get-tuple-element.415) | copy-start | bytes 1540
  174.0 24.5 %copy-start.10 = (f32[128]{0:T(128)S(1)}, f32[128]{0:T(128)}, u32[]{:S(2)}) copy-start(f32[128]{0:T(128)} %get-tuple-element.307) | copy-start | bytes 1540
  174.0 24.6 %copy-start.9 = (f32[128]{0:T(128)S(1)}, f32[128]{0:T(128)}, u32[]{:S(2)}) copy-start(f32[128]{0:T(128)} %get-tuple-element.308) | copy-start | bytes 1540
  174.0 24.7 %copy-start.8 = (f32[128]{0:T(128)S(1)}, f32[128]{0:T(128)}, u32[]{:S(2)}) copy-start(f32[128]{0:T(128)} %get-tuple-element.306) | copy-start | bytes 1540
  202.0 16.8 %copy-start.4 = (f32[4,64,2,128]{3,1,0,2:T(8,128)S(1)}, f32[4,64,2,128]{3,1,0,2:T(8,128)}, u32[]{:S(2)}) copy-start(f32[4,64,2,128]{3,1,0,2:T(8,128)} %get-tuple-element.144) | copy-start | bytes 786436
  221.5 21.8 %all-to-all-start.1 = ((bf16[4,256,256]{1,2,0:T(8,128)(2,1)}), bf16[4,256,256]{1,2,0:T(8,128)(2,1)S(1)}, u32[]{:S(2)}, u32[]{:S(2)}) async-start(bf16[4,256,256]{1,2,0:T(8,128)(2,1)} %stack.2), calls=%async_computation.1 | async-start | bytes 1048576 | tf_op jit(solution)/shard_map/all_to_all | solution.py:198
